TPU v7x, 32 devices: a whole 2x2x4 slice. The times are simulated.
32 devices in a mesh: expert: 4 (over z), shard: 8 (over y, x, core).
Axes of the slice: x: 2, y: 2, z: 4, core: 2. Of those that a mesh axis runs over, the one named last changes fastest.
Arguments:
- master_down: float32 [16, 6400, 4096], P('expert', None, 'shard'), may hold values from -0.109375 to 0.109375
- second_down: bfloat16 [16, 6400, 4096], P('expert', None, 'shard'), may hold values from -0.0390625 to 0.0390625
- router_weight: float32 [4096, 16], P('shard', 'expert'), may hold values from -0.09375 to 0.09375
- router_gain: float32 [4096], P('shard'), may hold values from 0.25 to 1.75
Outputs:
- final_down: bfloat16 [16, 6400, 4096], P('expert', 'shard')
- scale_down: float32 [16, 6400], P('expert', 'shard')
- serve_router: bfloat16 [4096, 16], replicated
All inputs are finite; a program needn't handle non-finite values.
Results may differ from a plain program's by a relative error of at most 0.001.
Values may be sent and summed in bfloat16 or wider, within the bound.
A program may use at most 256 MiB of HBM per device.

v0:
```python
import jax
import jax.numpy as jnp
from jax import lax
from jax.sharding import PartitionSpec as P


def local(master_down, second_down, router_weight, router_gain):
    merged_down = master_down + second_down.astype(jnp.float32)
    total_down = lax.psum(jnp.sum(merged_down * merged_down, axis=2), "shard")
    scale_down = jnp.sqrt(total_down)
    narrow_down = (merged_down / jnp.expand_dims(scale_down, 2)).astype(jnp.bfloat16)
    final_down = lax.all_to_all(narrow_down, "shard", split_axis=1, concat_axis=2, tiled=True)
    scale_down = lax.dynamic_slice_in_dim(
        scale_down, lax.axis_index("shard") * final_down.shape[1], final_down.shape[1], axis=1
    )
    part_router = (router_weight * router_gain[:, None]).astype(jnp.bfloat16)
    row_router = lax.all_gather(part_router, "shard", axis=0, tiled=True)
    serve_router = lax.all_gather(row_router, "expert", axis=1, tiled=True)
    return (final_down, scale_down, serve_router)


def solution(mesh):
    return jax.shard_map(
        local,
        mesh=mesh,
        in_specs=(
            P("expert", None, "shard"),
            P("expert", None, "shard"),
            P("shard", "expert"),
            P("shard"),
        ),
        out_specs=(P("expert", "shard", None), P("expert", "shard"), P()),
        check_vma=False,
    )
```

profile of v0, /device:TPU:0, one launch (start us, length us, event | category | flops | bytes accessed | tf_op | source)
XLA Modules:
  0.0 554.8 jit_solution(7517493062815123618)
XLA Ops:
  7.2 0.0 all-reduce.2.cloned.1.call-start
  7.2 24.2 %multiply_reduce_fusion = f32[4,6400]{1,0:T(4,128)S(1)} fusion(f32[4,6400,512]{2,1,0:T(8,128)} %param.4, bf16[4,6400,512]{2,1,0:T(8,128)(2,1)} %param.5), kind=kLoop, calls=%fused_computation.1 | loop fusion | flops 52403200 | bytes 78745600 | tf_op jit(solution)/shard_map/reduce_sum | solution.py:9
  31.4 2.3 copy.21
  33.7 0.0 all-reduce.2.cloned.1.call-update
  33.7 73.6 %all-reduce.2.cloned.1.call-done = f32[4,6400]{0,1:T(8,128)} async-done(((f32[4,6400]{0,1:T(8,128)}), f32[4,6400]{0,1:T(8,128)}) %all-reduce.2.cloned.1.call-update) | async-done | bytes 102416 | tf_op jit(solution)/shard_map/psum | solution.py:9
  107.3 2.7 sqrt.3
  110.0 1.2 copy.17
  111.3 34.3 %divide_convert_fusion = bf16[4,6400,512]{2,1,0:T(8,128)(2,1)} fusion(f32[4,6400,512]{2,1,0:T(8,128)} %param.4, bf16[4,6400,512]{2,1,0:T(8,128)(2,1)} %param.5, f32[4,6400]{1,0:T(4,128)S(1)} %copy.17), kind=kLoop, calls=%fused_computation | loop fusion | flops 52428800 | bytes 104960000 | tf_op jit(solution)/shard_map/convert_element_type | solution.py:11
  145.5 33.4 %copy.18 = bf16[4,6400,512]{2,0,1:T(4,128)(2,1)} copy(bf16[4,6400,512]{2,1,0:T(8,128)(2,1)} %divide_convert_fusion) | data formatting | bytes 52428800 | tf_op jit(solution)/shard_map/convert_element_type | solution.py:11
  178.9 0.0 copy-start
  178.9 0.0 copy-start.1
  178.9 6.6 %all-to-all-start = ((bf16[4,6400,512]{2,0,1:T(4,128)(2,1)}), bf16[4,6400,512]{2,0,1:T(4,128)(2,1)}, u32[]{:S(2)}, u32[]{:S(2)}) async-start(bf16[4,6400,512]{2,0,1:T(4,128)(2,1)} %copy.18), calls=%async_computation | async-start | bytes 52428800 | tf_op jit(solution)/shard_map/all_to_all | solution.py:12
  185.6 0.0 copy-done
  185.6 0.0 copy-done.1
  185.6 288.2 %all_gather.6 = bf16[4096,4]{0,1:T(4,128)(2,1)S(1)} all-gather(bf16[512,4]{0,1:T(4,128)(2,1)S(1)} %multiply_convert_fusion), channel_id=1, replica_groups=mesh['expert'=4,'shard'=8] {'shard'}, dimensions={0}, use_global_device_ids=true | all-gather | bytes 36864 | tf_op jit(solution)/shard_map/all_gather | solution.py:17
  473.8 13.5 %all-gather = bf16[4,4,4096]{2,1,0:T(4,128)(2,1)S(1)} all-gather(bf16[1,4,4096]{2,1,0:T(4,128)(2,1)S(1)} %bitcast.9), channel_id=1, replica_groups=mesh['expert'=4,'shard'=8] {'expert'}, dimensions={0}, use_global_device_ids=true | all-gather | bytes 163840 | tf_op jit(solution)/shard_map/all_gather | solution.py:18
  487.3 0.7 reshape.9
  488.0 0.8 constant_dynamic-slice_fusion
  488.7 1.8 copy.20
  490.5 0.0 all-to-all-done
  490.5 18.2 %copy.19 = bf16[4,800,8,512]{3,2,1,0:T(8,128)(2,1)} copy(bf16[4,800,8,512]{3,0,1,2:T(4,128)(2,1)} %bitcast.1) | data formatting | bytes 52428800 | tf_op jit(solution)/shard_map/all_to_all | solution.py:12
  508.7 39.2 %all_to_all.16 = bf16[4,800,4096]{2,1,0:T(8,128)(2,1)} reshape(bf16[4,800,8,512]{3,2,1,0:T(8,128)(2,1)} %copy.19) | data formatting | bytes 52428800 | tf_op jit(solution)/shard_map/all_to_all | solution.py:12
  (1 shorter events, 0.0 us)
Async XLA Ops:
  7.2 100.2 %all-reduce.2.cloned.1.call-start = ((), (), s32[]{:S(2)}) async-start(), calls=%async_computation.1 | async-start | bytes 6553600 | tf_op jit(solution)/shard_map/psum | solution.py:9
  178.9 6.7 %copy-start = (f32[512,4]{0,1:T(4,128)S(1)}, f32[512,4]{0,1:T(4,128)}, u32[]{:S(2)}) copy-start(f32[512,4]{0,1:T(4,128)} %param.6) | copy-start | bytes 24580
  178.9 6.7 %copy-start.1 = (f32[512]{0:T(512)S(1)}, f32[512]{0:T(512)}, u32[]{:S(2)}) copy-start(f32[512]{0:T(512)} %param.7) | copy-start | bytes 6148
  178.9 311.6 %all-to-all-start = ((bf16[4,6400,512]{2,0,1:T(4,128)(2,1)}), bf16[4,6400,512]{2,0,1:T(4,128)(2,1)}, u32[]{:S(2)}, u32[]{:S(2)}) async-start(bf16[4,6400,512]{2,0,1:T(4,128)(2,1)} %copy.18), calls=%async_computation | async-start | bytes 52428800 | tf_op jit(solution)/shard_map/all_to_all | solution.py:12
Sparse Core Ops, SparseCore 0:
  33.9 73.4 all-reduce.1
where the time goes:
time: 556 us; the launch traced here: 555 us
  blocking collectives  302 us (54%)
  local copies, waits for them, and re-layouts  100 us (18%)
  waiting for transfers between devices  73.6 us (13%)
  other arithmetic  58.5 us (11%)
  between operations  14.1 us (3%)
  starting transfers between devices  6.67 us (1%)
    all_gather x1, blocking collectives, local(): row_router = lax.all_gather(part_router, 'shard', axis=0, tiled=True)  288 us
    psum x1, waiting for transfers between devices, local(): total_down = lax.psum(jnp.sum(merged_down * merged_down, axis=2), 'shard')  73.6 us
    all_to_all x2, local copies, waits for them, and re-layouts, local(): lax.all_to_all(narrow_down, 'shard', split_axis=1, concat_axis=2, tiled=T...  57.4 us
    convert_element_type x1, other arithmetic, local(): (merged_down / jnp.expand_dims(scale_down, 2)).astype(jnp.bfloat16)  34.3 us
    convert_element_type x1, local copies, waits for them, and re-layouts, local(): (merged_down / jnp.expand_dims(scale_down, 2)).astype(jnp.bfloat16)  33.4 us
    reduce_sum x1, other arithmetic, local(): total_down = lax.psum(jnp.sum(merged_down * merged_down, axis=2), 'shard')  24.2 us
    all_gather x1, blocking collectives, local(): serve_router = lax.all_gather(row_router, 'expert', axis=1, tiled=True)  13.5 us
  transfers between devices with their start and end apart: 2, of which 1 were waited for; matrix products, arithmetic and copies ran while one was open for 1% of the time, Pallas kernels for 0%

commit v1 on v0

v1 whole, which is shorter than its diff:
```python
import functools

import jax
import jax.numpy as jnp
from jax import lax
from jax.experimental import pallas as pl
from jax.experimental.pallas import tpu as pltpu
from jax.sharding import PartitionSpec as P

MESH = pl.DeviceIdType.MESH
QUEUE = 3
READS = 3
SKEW = 2


def rows_per_chunk(rows):
    return max(r for r in range(16, 129, 16) if rows % r == 0)


def flipped(index, mask):
    out, bit = 0, 1
    while bit <= mask:
        own = lax.rem(index // bit, 2)
        if mask & bit:
            out = out + bit * (1 - 2 * own)
        bit *= 2
    return index + out


def kernel(
    shards, groups, master, second, weight, gain,
    final, scale, router,
    sum_master, sum_second, norm_master, norm_second, ready,
    part, landed, rpart, rall,
    sum_sems, norm_sems, send_sems, own_sems, final_sems,
    part_send, part_recv, rsend, rrecv, gsend, grecv,
):
    experts, _, rows, cols = master.shape
    take = rows_per_chunk(rows)
    blocks = rows // take
    chunks = experts * blocks
    stages = shards.bit_length() - 1
    me = lax.axis_index("shard")
    group = lax.axis_index("expert")
    lag = SKEW * stages

    def reads(k, bufs, sems):
        slot = lax.rem(k, READS)
        e, b = k // blocks, lax.rem(k, blocks)
        where = pl.ds(pl.multiple_of(b * take, 16), take)
        return [
            pltpu.make_async_copy(src.at[e, :, where, :], buf.at[slot], sems.at[i, slot])
            for i, (src, buf) in enumerate(zip((master, second), bufs))
        ]

    sum_bufs, norm_bufs = (sum_master, sum_second), (norm_master, norm_second)

    for k in range(min(READS, chunks)):
        for c in reads(k, sum_bufs, sum_sems):
            c.start()

    barrier = pltpu.get_barrier_semaphore()
    for o in range(1, shards):
        pl.semaphore_signal(barrier, inc=1, device_id={"shard": flipped(me, o)}, device_id_type=MESH)
    for o in range(1, groups):
        pl.semaphore_signal(barrier, inc=1, device_id={"expert": lax.rem(group + o, groups)}, device_id_type=MESH)

    product = (weight[...] * gain[...]).astype(jnp.bfloat16)
    rpart[...] = product
    mine = pl.ds(pl.multiple_of(me * cols, 128), cols)
    rall[group, :, mine] = product
    for k in range(min(READS, chunks)):
        for c in reads(k, norm_bufs, norm_sems):
            c.start()
    pl.semaphore_wait(barrier, shards + groups - 2)

    def exchange(stage, k):
        return pltpu.make_async_remote_copy(
            src_ref=part.at[stage, k],
            dst_ref=landed.at[stage, k],
            send_sem=part_send.at[stage],
            recv_sem=part_recv.at[stage, k],
            device_id={"shard": flipped(me, 1 << stage)},
            device_id_type=MESH,
        )

    eye = lax.broadcasted_iota(jnp.int32, (take, 128), 0) == lax.broadcasted_iota(jnp.int32, (take, 128), 1)

    def send(k, o):
        slot = lax.rem(k, QUEUE)
        e, b = k // blocks, lax.rem(k, blocks)
        where = pl.ds(pl.multiple_of(b * take, 16), take)
        to = flipped(me, o)
        return pltpu.make_async_remote_copy(
            src_ref=ready.at[slot, to],
            dst_ref=final.at[e, where, mine],
            send_sem=send_sems.at[slot],
            recv_sem=final_sems.at[me],
            device_id={"shard": to},
            device_id_type=MESH,
        )

    def keep(k):
        slot = lax.rem(k, QUEUE)
        e, b = k // blocks, lax.rem(k, blocks)
        where = pl.ds(pl.multiple_of(b * take, 16), take)
        return pltpu.make_async_copy(ready.at[slot, me], final.at[e, where, mine], own_sems.at[slot])

    def drain(k):
        slot = lax.rem(k, QUEUE)
        several = ready.at[slot, pl.ds(0, shards - 1)]
        pltpu.make_async_copy(several, several, send_sems.at[slot]).wait()
        keep(k).wait()

    def tick(t, carry):
        @pl.when(t < chunks)
        def _():
            slot = lax.rem(t, READS)
            for c in reads(t, sum_bufs, sum_sems):
                c.wait()

            def one(d, carry):
                x = sum_master[slot, d] + sum_second[slot, d].astype(jnp.float32)
                column = jnp.sum(x * x, axis=1, keepdims=True)
                part[0, t, pl.ds(d, 1), :] = jnp.sum(jnp.where(eye, column, 0.0), axis=0, keepdims=True)
                return carry

            lax.fori_loop(0, shards, one, 0, unroll=2)

            @pl.when(t + READS < chunks)
            def _():
                for c in reads(t + READS, sum_bufs, sum_sems):
                    c.start()

        for stage in range(1, stages):
            k = t - SKEW * stage

            @pl.when((k >= 0) & (k < chunks))
            def _():
                exchange(stage - 1, k).wait_recv()
                part[stage, k] = part[stage - 1, k] + landed[stage - 1, k]

        for stage in range(stages):
            k = t - SKEW * stage

            @pl.when((k >= 0) & (k < chunks))
            def _():
                exchange(stage, k).start()

        k = t - lag

        @pl.when((k >= 0) & (k < chunks))
        def _():
            slot = lax.rem(k, READS)
            out = lax.rem(k, QUEUE)
            exchange(stages - 1, k).wait_recv()
            part[stages, k] = jnp.sqrt(part[stages - 1, k] + landed[stages - 1, k])
            scale[pl.ds(k, 1), :] = part[stages, k, pl.ds(me, 1), :]
            for c in reads(k, norm_bufs, norm_sems):
                c.wait()

            @pl.when(k >= QUEUE)
            def _():
                drain(k - QUEUE)

            def one(d, carry):
                row = 1.0 / part[stages, k, pl.ds(d, 1), :]
                column = jnp.sum(jnp.where(eye, row, 0.0), axis=1, keepdims=True)
                x = norm_master[slot, d] + norm_second[slot, d].astype(jnp.float32)
                ready[out, d] = (x * column).astype(jnp.bfloat16)
                return carry

            lax.fori_loop(0, shards, one, 0, unroll=2)

            @pl.when(k + READS < chunks)
            def _():
                for c in reads(k + READS, norm_bufs, norm_sems):
                    c.start()

            for o in range(shards - 1, 0, -1):
                send(k, o).start()
            keep(k).start()

        return carry

    def rows_copy(o):
        return pltpu.make_async_remote_copy(
            src_ref=rpart,
            dst_ref=rall.at[group, :, mine],
            send_sem=rsend,
            recv_sem=rrecv.at[me],
            device_id={"shard": flipped(me, o)},
            device_id_type=MESH,
        )

    for o in range(1, shards):
        rows_copy(o).start()

    lax.fori_loop(0, chunks + lag, tick, 0)

    def group_copy(o):
        return pltpu.make_async_remote_copy(
            src_ref=rall.at[group],
            dst_ref=rall.at[group],
            send_sem=gsend.at[o],
            recv_sem=grecv.at[group],
            device_id={"expert": lax.rem(group + o, groups)},
            device_id_type=MESH,
        )

    for o in range(1, shards):
        rows_copy(o).wait_send()
        other = flipped(me, o)
        there = rall.at[group, :, pl.ds(pl.multiple_of(other * cols, 128), cols)]
        pltpu.make_async_copy(there, there, rrecv.at[other]).wait()
    for o in range(1, groups):
        group_copy(o).start()
    for o in range(1, groups):
        other = lax.rem(group + o, groups)
        pltpu.make_async_copy(rall.at[other], rall.at[other], grecv.at[other]).wait()
        group_copy(o).wait_send()
    router[...] = rall[...]

    for stage in range(stages):
        pltpu.make_async_copy(part.at[stage], part.at[stage], part_send.at[stage]).wait()
    for k in range(max(0, chunks - QUEUE), chunks):
        drain(k)
    for o in range(1, shards):
        other = flipped(me, o)
        there = final.at[:, :, pl.ds(pl.multiple_of(other * cols, 128), cols)]
        pltpu.make_async_copy(there, there, final_sems.at[other]).wait()


def local(shards, groups, master_down, second_down, router_weight, router_gain):
    experts, d_expert, cols = master_down.shape
    rows = d_expert // shards
    take = rows_per_chunk(rows)
    chunks = experts * (rows // take)
    stages = shards.bit_length() - 1
    gcols = router_weight.shape[1]
    f32, bf16 = jnp.float32, jnp.bfloat16
    final, scale, router = pl.pallas_call(
        functools.partial(kernel, shards, groups),
        out_shape=(
            jax.ShapeDtypeStruct((experts, rows, cols * shards), bf16),
            jax.ShapeDtypeStruct((chunks, 128), f32),
            jax.ShapeDtypeStruct((groups, gcols, cols * shards), bf16),
        ),
        in_specs=[pl.BlockSpec(memory_space=pl.ANY)] * 2 + [pl.BlockSpec(memory_space=pltpu.VMEM)] * 2,
        out_specs=(
            pl.BlockSpec(memory_space=pl.ANY),
            pl.BlockSpec(memory_space=pltpu.VMEM),
            pl.BlockSpec(memory_space=pltpu.VMEM),
        ),
        scratch_shapes=[
            pltpu.VMEM((READS, shards, take, cols), f32),
            pltpu.VMEM((READS, shards, take, cols), bf16),
            pltpu.VMEM((READS, shards, take, cols), f32),
            pltpu.VMEM((READS, shards, take, cols), bf16),
            pltpu.VMEM((QUEUE, shards, take, cols), bf16),
            pltpu.VMEM((stages + 1, chunks, shards, 128), f32),
            pltpu.VMEM((stages, chunks, shards, 128), f32),
            pltpu.VMEM((gcols, cols), bf16),
            pltpu.VMEM((groups, gcols, cols * shards), bf16),
            pltpu.SemaphoreType.DMA((2, READS)),
            pltpu.SemaphoreType.DMA((2, READS)),
            pltpu.SemaphoreType.DMA((QUEUE,)),
            pltpu.SemaphoreType.DMA((QUEUE,)),
            pltpu.SemaphoreType.DMA((shards,)),
            pltpu.SemaphoreType.DMA((stages,)),
            pltpu.SemaphoreType.DMA((stages, chunks)),
            pltpu.SemaphoreType.DMA,
            pltpu.SemaphoreType.DMA((shards,)),
            pltpu.SemaphoreType.DMA((groups,)),
            pltpu.SemaphoreType.DMA((groups,)),
        ],
        compiler_params=pltpu.CompilerParams(collective_id=0, has_side_effects=True, vmem_limit_bytes=32 * 2**20),
    )(
        master_down.reshape(experts, shards, rows, cols),
        second_down.reshape(experts, shards, rows, cols),
        router_weight.T,
        router_gain[None, :],
    )
    scale = scale[:, :take].reshape(experts, rows)
    return (final, scale, router.reshape(groups * gcols, cols * shards).T)


def solution(mesh):
    shards, groups = mesh.shape["shard"], mesh.shape["expert"]
    return jax.shard_map(
        functools.partial(local, shards, groups),
        mesh=mesh,
        in_specs=(
            P("expert", None, "shard"),
            P("expert", None, "shard"),
            P("shard", "expert"),
            P("shard"),
        ),
        out_specs=(P("expert", "shard", None), P("expert", "shard"), P()),
        check_vma=False,
    )
```

time: 556 us -> 321 us (0.58)
  blocking collectives: 302 us -> 0 us
  Pallas kernels: 0 us -> 300 us
  local copies, waits for them, and re-layouts: 100 us -> 20.7 us
  waiting for transfers between devices: 73.6 us -> 0 us
  other arithmetic: 58.5 us -> 0 us
  between operations: 14.1 us -> 0.65 us
  starting transfers between devices: 6.67 us -> 0 us
    all_gather x2 -> x0, blocking collectives: 302 us -> none  [the longest x1 288 us: local(): row_router = lax.all_gather(part_router, 'shard', axis=0, tiled=True)]
    pallas_call x0 -> x1, Pallas kernels: none -> 300 us  [local(): pl.pallas_call(functools.partial(kernel, shards, groups), out_shape=(jax....]
    psum x1 -> x0, waiting for transfers between devices: 73.6 us -> none  [local(): total_down = lax.psum(jnp.sum(merged_down * merged_down, axis=2), 'shard')]
    all_to_all x2 -> x0, local copies, waits for them, and re-layouts: 57.4 us -> none  [local(): lax.all_to_all(narrow_down, 'shard', split_axis=1, concat_axis=2, tiled=T...]
    convert_element_type x2 -> x0, other arithmetic: 34.3 us -> none  [the longest x1 34.3 us: local(): (merged_down / jnp.expand_dims(scale_down, 2)).astype(jnp.bfloat16)]
    convert_element_type x1 -> x0, local copies, waits for them, and re-layouts: 33.4 us -> none  [local(): (merged_down / jnp.expand_dims(scale_down, 2)).astype(jnp.bfloat16)]
    reduce_sum x1 -> x0, other arithmetic: 24.2 us -> none  [local(): total_down = lax.psum(jnp.sum(merged_down * merged_down, axis=2), 'shard')]
    unnamed x7 -> x5, local copies, waits for them, and re-layouts: 4.75 us -> 19.3 us
  transfers between devices with their start and end apart: 2 -> 0, of which waited for: 1 -> 0; matrix products, arithmetic and copies ran while one was open for 1% -> 0% of each run, Pallas kernels for 0% -> 0%
where the time goes in v1:
time: 321 us
  Pallas kernels  300 us (93%)
  local copies, waits for them, and re-layouts  20.7 us (6%)
    pallas_call x1, Pallas kernels, local(): pl.pallas_call(functools.partial(kernel, shards, groups), out_shape=(jax....  300 us
    unnamed x5, local copies, waits for them, and re-layouts  19.3 us

profile of v1, /device:TPU:0, one launch (start us, length us, event | category | flops | bytes accessed | tf_op | source)
XLA Modules:
  0.0 321.0 jit_solution(11032793400067985503)
XLA Ops:
  0.6 0.0 copy-start
  0.6 0.7 copy-done
  1.3 0.0 copy-start.1
  1.3 0.7 copy-done.1
  2.0 299.6 %shard_map.67 = (bf16[4,800,4096]{2,1,0:T(8,128)(2,1)}, f32[40,128]{1,0:T(8,128)S(1)}, bf16[4,4,4096]{2,1,0:T(4,128)(2,1)S(1)}) custom-call(f32[4,8,800,512]{3,2,1,0:T(8,128)} %bitcast.9, bf16[4,8,800,512]{3,2,1,0:T(8,128)(2,1)} %bitcast.10, f32[4,512]{1,0:T(4,128)S(1)} %bitcast.7, f32[1,512]{1,0:T(1,128)S(1)} %bitcast.8), custom_call_target="tpu_custom_call" | custom-call | tf_op jit(solution)/shard_map/pallas_call | solution.py:242
  301.6 0.7 reshape.20
  302.3 0.7 reshape.21
  303.0 17.9 %copy.8 = bf16[4,800,4096]{2,1,0:T(8,128)(2,1)} copy(bf16[4,800,4096]{2,1,0:T(8,128)(2,1)} %get-tuple-element.12) | data formatting | bytes 52428800
Async XLA Ops:
  0.6 0.7 copy-start
  1.3 0.7 copy-start.1

commit v2 on v1

--- a/solution.py
+++ b/solution.py
@@ -10,7 +10,7 @@
 MESH = pl.DeviceIdType.MESH
 QUEUE = 3
 READS = 3
-SKEW = 2
+SKEW = 1
 
 
 def rows_per_chunk(rows):
@@ -34,6 +34,7 @@
     part, landed, rpart, rall,
     sum_sems, norm_sems, send_sems, own_sems, final_sems,
     part_send, part_recv, rsend, rrecv, gsend, grecv,
+    weight_here, gain_here, small_sems,
 ):
     experts, _, rows, cols = master.shape
     take = rows_per_chunk(rows)
@@ -59,13 +60,21 @@
         for c in reads(k, sum_bufs, sum_sems):
             c.start()
 
+    small = [
+        pltpu.make_async_copy(weight, weight_here, small_sems.at[0]),
+        pltpu.make_async_copy(gain, gain_here, small_sems.at[1]),
+    ]
+    for c in small:
+        c.start()
     barrier = pltpu.get_barrier_semaphore()
     for o in range(1, shards):
         pl.semaphore_signal(barrier, inc=1, device_id={"shard": flipped(me, o)}, device_id_type=MESH)
     for o in range(1, groups):
         pl.semaphore_signal(barrier, inc=1, device_id={"expert": lax.rem(group + o, groups)}, device_id_type=MESH)
 
-    product = (weight[...] * gain[...]).astype(jnp.bfloat16)
+    for c in small:
+        c.wait()
+    product = (weight_here[...] * gain_here[...]).astype(jnp.bfloat16)
     rpart[...] = product
     mine = pl.ds(pl.multiple_of(me * cols, 128), cols)
     rall[group, :, mine] = product
@@ -246,7 +255,7 @@
             jax.ShapeDtypeStruct((chunks, 128), f32),
             jax.ShapeDtypeStruct((groups, gcols, cols * shards), bf16),
         ),
-        in_specs=[pl.BlockSpec(memory_space=pl.ANY)] * 2 + [pl.BlockSpec(memory_space=pltpu.VMEM)] * 2,
+        in_specs=[pl.BlockSpec(memory_space=pl.ANY)] * 2 + [pl.BlockSpec(memory_space=pltpu.HBM)] * 2,
         out_specs=(
             pl.BlockSpec(memory_space=pl.ANY),
             pl.BlockSpec(memory_space=pltpu.VMEM),
@@ -273,6 +282,9 @@
             pltpu.SemaphoreType.DMA((shards,)),
             pltpu.SemaphoreType.DMA((groups,)),
             pltpu.SemaphoreType.DMA((groups,)),
+            pltpu.VMEM((gcols, cols), f32),
+            pltpu.VMEM((1, cols), f32),
+            pltpu.SemaphoreType.DMA((2,)),
         ],
         compiler_params=pltpu.CompilerParams(collective_id=0, has_side_effects=True, vmem_limit_bytes=32 * 2**20),
     )(

time: 321 us -> 321 us (level)
  no operation moved by 1% of the time
where the time goes in v2:
time: 321 us
  Pallas kernels  299 us (93%)
  local copies, waits for them, and re-layouts  20.7 us (6%)
    pallas_call x1, Pallas kernels, local(): pl.pallas_call(functools.partial(kernel, shards, groups), out_shape=(jax....  299 us
    unnamed x5, local copies, waits for them, and re-layouts  19.3 us

profile of v2, /device:TPU:0, one launch (start us, length us, event | category | flops | bytes accessed | tf_op | source)
XLA Modules:
  0.0 320.6 jit_solution(17256772812710226369)
XLA Ops:
  0.6 0.0 copy-start
  0.6 0.7 copy-done
  1.3 0.0 copy-start.1
  1.3 0.7 copy-done.1
  2.0 299.3 %shard_map.67 = (bf16[4,800,4096]{2,1,0:T(8,128)(2,1)}, f32[40,128]{1,0:T(8,128)S(1)}, bf16[4,4,4096]{2,1,0:T(4,128)(2,1)S(1)}) custom-call(f32[4,8,800,512]{3,2,1,0:T(8,128)} %bitcast.9, bf16[4,8,800,512]{3,2,1,0:T(8,128)(2,1)} %bitcast.10, f32[4,512]{1,0:T(4,128)S(1)} %bitcast.7, f32[1,512]{1,0:T(1,128)S(1)} %bitcast.8), custom_call_target="tpu_custom_call" | custom-call | tf_op jit(solution)/shard_map/pallas_call | solution.py:251
  301.3 0.7 reshape.20
  302.0 0.7 reshape.21
  302.7 17.9 %copy.8 = bf16[4,800,4096]{2,1,0:T(8,128)(2,1)} copy(bf16[4,800,4096]{2,1,0:T(8,128)(2,1)} %get-tuple-element.12) | data formatting | bytes 52428800
Async XLA Ops:
  0.6 0.7 copy-start
  1.3 0.7 copy-start.1
